TPU v7x, 32 devices: a whole 2x2x4 slice. The times are simulated.
32 devices in a mesh: layer: 8 (over z, x), split: 4 (over y, core).
Axes of the slice: x: 2, y: 2, z: 4, core: 2. Of those that a mesh axis runs over, the one named last changes fastest.
Arguments:
- right_side: float32 [32, 512, 128], P('layer', 'split'), may hold values from -6 to 6
- diagonal: float32 [32, 512, 128], P('layer', 'split'), may hold values from 0.1 to 1
- inverses: float32 [32, 512, 512], P('layer', None, 'split'), may hold values from -1 to 1, as said below
Outputs:
- solution_field: float32 [32, 512, 128], P('layer', 'split')
- residual: float32 [32, 512, 128], P('layer', 'split')
Inputs may be any that keep to these rules, and one draw needn't show every extreme that they name: `inverses`: each plane's inverse is a diagonal matrix with entries between 0.5 and 1 plus a dense coupling with zero diagonal and spectral norm below 0.2.
All inputs are finite; a program needn't handle non-finite values.
Results may differ from a plain program's by a relative error of at most 0.0003.
Values sent between devices are 32-bit elements; how exact they have to be, the bound alone decides.
No kernel may reach another device: no remote copies, remote signals or barrier semaphores. Data moves between devices by JAX's collectives and lax.ppermute only.
A program may use at most 64 MiB of HBM per device.

v0:
```python
import jax
import jax.numpy as jnp
from jax import lax
from jax.sharding import PartitionSpec as P


def with_halo(x, sides, width):
    for axis, dim in sides:
        size, length = (lax.axis_size(axis), x.shape[dim])
        up = [(i, (i + 1) % size) for i in range(size - 1)]
        down = [(j, i) for i, j in up]
        last = lax.slice_in_dim(x, length - width, length, axis=dim)
        first = lax.slice_in_dim(x, 0, width, axis=dim)
        before = lax.ppermute(last, axis, up)
        after = lax.ppermute(first, axis, down)
        x = jnp.concatenate([before, x, after], axis=dim)
    return x


def from_behind(block, axis, distance):
    devices = range(lax.axis_size(axis))
    route = [(i - distance, i) for i in devices if i - distance in devices]
    return lax.ppermute(block, axis, route)


def stencil(values, diagonal):
    padded = with_halo(values, (("layer", 0), ("split", 1)), 1)
    beside = padded[2:, 1:-1, :] + padded[:-2, 1:-1, :]
    beside = beside + padded[1:-1, 2:, :] + padded[1:-1, :-2, :]
    centre_part = padded[1:-1, 1:-1, :]
    y_upper = jnp.pad(centre_part[:, :, 1:], ((0, 0), (0, 0), (0, 1)))
    y_lower = jnp.pad(centre_part[:, :, :-1], ((0, 0), (0, 0), (1, 0)))
    return (6.0 + diagonal) * values - beside - y_upper - y_lower


def down_local(matrices, portion, carried):

    def down_advance(state, inputs):
        matrix, source = inputs
        state = jnp.dot(matrix, source + state, precision=lax.Precision.HIGHEST)
        return (state, state)

    return lax.scan(down_advance, carried, (matrices, portion))


def up_local(matrices, portion, carried):

    def up_advance(state, inputs):
        matrix, below = inputs
        state = below + jnp.dot(matrix, state, precision=lax.Precision.HIGHEST)
        return (state, state)

    return lax.scan(up_advance, carried, (matrices, portion), reverse=True)


def chain_sweep(sweep_fn, matrices, source, sender, anchor, nblocks):
    depth_count = lax.axis_size("layer")
    block_width = source.shape[2] // nblocks
    plane_shape = (source.shape[1], block_width)
    result = jnp.zeros_like(source)
    incoming = jnp.zeros(plane_shape, jnp.float32)

    def chain_advance(turn, state):
        result, incoming = state
        block_raw = turn - anchor
        active = jnp.logical_and(block_raw >= 0, block_raw < nblocks)

        def working(unused):
            return sweep_fn(matrices, source, incoming)

        def resting(unused):
            return (jnp.zeros(plane_shape, jnp.float32), jnp.zeros_like(source))

        outgoing, stacked = lax.cond(active, working, resting, None)
        previous = result
        result = jnp.where(active, stacked, previous)
        return (result, sender(outgoing))

    result, incoming = lax.fori_loop(
        0, depth_count + nblocks - 1, chain_advance, (result, incoming)
    )
    return result


def per_device(right_side, diagonal, inverses):
    matrices = lax.all_gather(inverses, "split", axis=2, tiled=True)
    columns = lax.all_to_all(right_side, "split", split_axis=2, concat_axis=1, tiled=True)
    nblocks = 1
    own_index = lax.axis_index("layer")
    depth_count = lax.axis_size("layer")
    applied_rhs = stencil(right_side, diagonal)

    def send_down(values):
        return from_behind(values, "layer", 1)

    def send_up(values):
        return from_behind(values, "layer", -1)

    lower_sweep = chain_sweep(down_local, matrices, columns, send_down, own_index, nblocks)
    upper_sweep = chain_sweep(
        up_local, matrices, lower_sweep, send_up, depth_count - 1 - own_index, nblocks
    )
    direction = lax.all_to_all(upper_sweep, "split", split_axis=1, concat_axis=2, tiled=True)
    image = stencil(direction, diagonal)
    applied_image = stencil(image, diagonal)
    sums_all = lax.psum(
        (
            jnp.sum(right_side * right_side),
            jnp.sum(right_side * image),
            jnp.sum(applied_rhs * right_side),
            jnp.sum(applied_rhs * image),
            jnp.sum(applied_image * right_side),
            jnp.sum(applied_image * image),
            jnp.sum(applied_rhs * applied_rhs),
            jnp.sum(applied_rhs * applied_image),
            jnp.sum(applied_image * applied_image),
        ),
        ("layer", "split"),
    )
    (
        norm_sq,
        curv_sum,
        rhs_rhs,
        rhs_image,
        image_rhs,
        image_image,
        arhs_arhs,
        arhs_aimage,
        aimage_aimage,
    ) = sums_all
    step_alpha = norm_sq / curv_sum
    middle = right_side - step_alpha * image
    tangent = applied_rhs - step_alpha * applied_image
    cross_sum = (
        rhs_rhs - step_alpha * (rhs_image + image_rhs) + step_alpha * step_alpha * image_image
    )
    self_sum = arhs_arhs - 2.0 * step_alpha * arhs_aimage + step_alpha * step_alpha * aimage_aimage
    step_omega = cross_sum / self_sum
    solution_field = step_alpha * direction + step_omega * middle
    residual = middle - step_omega * tangent
    return (solution_field, residual)


def solution(mesh):
    placed = (P("layer", "split", None), P("layer", "split", None), P("layer", None, "split"))
    return jax.shard_map(
        per_device,
        mesh=mesh,
        in_specs=placed,
        out_specs=(P("layer", "split", None), P("layer", "split", None)),
        check_vma=False,
    )
```

profile of v0, /device:TPU:12, one launch (start us, length us, event | category | flops | bytes accessed | tf_op | source)
XLA Modules:
  0.0 438.9 jit_solution(2182941142321325081)
XLA Ops:
  7.9 1.8 copy.44
  9.7 3.9 all-to-all-start
  14.7 3.3 collective-permute-start.6
  18.0 2.6 collective-permute-start.7
  23.4 21.4 %all-gather.2.cloned.1.call-done = f32[4,512,512]{2,1,0:T(8,128)} async-done(((f32[4,512,128]{2,1,0:T(8,128)}), f32[4,512,512]{2,1,0:T(8,128)}) %all-gather.2.cloned.1.call-update) | async-done | bytes 4194320 | tf_op jit(solution)/shard_map/all_gather | solution.py:86
  44.8 112.2 %while.60 = (s32[]{:T(128)}, f32[4,512,32]{1,2,0:T(8,128)S(1)}, f32[512,32]{0,1:T(8,128)S(1)}, s32[]{:T(128)}, f32[4,512,512]{2,1,0:T(8,128)}, /*index=5*/f32[4,512,32]{1,2,0:T(8,128)S(1)}, s32[]{:T(128)}, s32[]{:T(128)}) while((s32[]{:T(128)}, f32[4,512,32]{1,2,0:T(8,128)S(1)}, f32[512,32]{0,1:T(8,128)S(1)}, s32[]{:T(128)}, ...), condition=%wide.region_7.8_spmd.clone, body=%wide.region_2.7_spmd.clone.sunk | while | flops 100810760 | bytes 2623315 | solution.py:79
  45.5 3.4 collective-permute-start.1
  49.0 3.6 collective-permute-done.1
  53.3 2.5 collective-permute-start.1
  55.9 22.0 %collective-permute-done.1 = f32[512,32]{0,1:T(8,128)S(1)} collective-permute-done((f32[512,32]{0,1:T(8,128)S(1)}, f32[512,32]{0,1:T(8,128)S(1)}, u32[]{:S(2)}, u32[]{:S(2)}) %collective-permute-start.1) | collective-permute-done | bytes 65568 | tf_op jit(solution)/shard_map/while/body/eval_jaxpr/ppermute | solution.py:23
  77.9 11.7 %conditional.6 = (f32[512,32]{0,1:T(8,128)S(1)}, f32[4,512,32]{1,2,0:T(8,128)}) conditional(s32[]{:T(128)} %convert_element_type.26, () %tuple.150, (f32[4,512,512]{2,1,0:T(8,128)}, f32[4,512,32]{1,2,0:T(8,128)S(1)}, f32[512,32]{0,1:T(8,128)S(1)}) %tuple.151), branch_computations={%region_3.3_spmd, %region_4.6_spmd} | conditional | flops 100679680 | bytes 1574541 | solution.py:74
  77.9 11.7 %while.58 = (s32[]{:T(128)}, f32[512,32]{0,1:T(8,128)S(1)}, f32[4,512,32]{1,2,0:T(8,128)}, f32[4,512,512]{2,1,0:T(8,128)}, f32[4,512,32]{1,2,0:T(8,128)S(1)}, /*index=5*/s32[]{:T(128)}) while((s32[]{:T(128)}, f32[512,32]{0,1:T(8,128)S(1)}, f32[4,512,32]{1,2,0:T(8,128)}, f32[4,512,512]{2,1,0:T(8,128)}, f32[4,512,32]{1,2,0:T(8,128)S(1)}, ...), condition=%wide.region_6.5_spmd, body=%wide.region_5.4_spmd.sunk | while | flops 100679680 | bytes 1443397 | solution.py:43
  77.9 2.9 bitcast_dynamic-update-slice_fusion.5
  80.8 2.9 bitcast_dynamic-update-slice_fusion.5
  83.8 2.9 bitcast_dynamic-update-slice_fusion.5
  86.7 2.9 bitcast_dynamic-update-slice_fusion.5
  89.6 1.9 collective-permute-start.1
  92.6 4.1 collective-permute-done.1
  97.4 12.0 %collective-permute-start.1 = (f32[512,32]{0,1:T(8,128)S(1)}, f32[512,32]{0,1:T(8,128)S(1)}, u32[]{:S(2)}, u32[]{:S(2)}) collective-permute-start(f32[512,32]{0,1:T(8,128)S(1)} %get-tuple-element.643), channel_id=1, source_target_pairs={{0,4},{4,8},{8,12},{12,16},{16,20},{20,24},{24,28},{1,5},{5,9},{9,... | collective-permute-start | bytes 196616 | tf_op jit(solution)/shard_map/while/body/eval_jaxpr/ppermute | solution.py:23
  109.5 1.8 collective-permute-done.1
  112.0 4.3 collective-permute-start.1
  116.4 2.7 collective-permute-done.1
  119.8 12.9 %collective-permute-start.1 = (f32[512,32]{0,1:T(8,128)S(1)}, f32[512,32]{0,1:T(8,128)S(1)}, u32[]{:S(2)}, u32[]{:S(2)}) collective-permute-start(f32[512,32]{0,1:T(8,128)S(1)} %get-tuple-element.643), channel_id=1, source_target_pairs={{0,4},{4,8},{8,12},{12,16},{16,20},{20,24},{24,28},{1,5},{5,9},{9,... | collective-permute-start | bytes 196616 | tf_op jit(solution)/shard_map/while/body/eval_jaxpr/ppermute | solution.py:23
  135.3 5.2 %collective-permute-start.1 = (f32[512,32]{0,1:T(8,128)S(1)}, f32[512,32]{0,1:T(8,128)S(1)}, u32[]{:S(2)}, u32[]{:S(2)}) collective-permute-start(f32[512,32]{0,1:T(8,128)S(1)} %get-tuple-element.643), channel_id=1, source_target_pairs={{0,4},{4,8},{8,12},{12,16},{16,20},{20,24},{24,28},{1,5},{5,9},{9,... | collective-permute-start | bytes 196616 | tf_op jit(solution)/shard_map/while/body/eval_jaxpr/ppermute | solution.py:23
  143.1 12.0 %collective-permute-start.1 = (f32[512,32]{0,1:T(8,128)S(1)}, f32[512,32]{0,1:T(8,128)S(1)}, u32[]{:S(2)}, u32[]{:S(2)}) collective-permute-start(f32[512,32]{0,1:T(8,128)S(1)} %get-tuple-element.643), channel_id=1, source_target_pairs={{0,4},{4,8},{8,12},{12,16},{16,20},{20,24},{24,28},{1,5},{5,9},{9,... | collective-permute-start | bytes 196616 | tf_op jit(solution)/shard_map/while/body/eval_jaxpr/ppermute | solution.py:23
  157.0 155.7 %while.61 = (s32[]{:T(128)}, f32[4,512,32]{1,2,0:T(8,128)S(1)}, f32[512,32]{0,1:T(8,128)S(1)}, s32[]{:T(128)}, f32[4,512,32]{1,2,0:T(8,128)S(1)}, /*index=5*/f32[4,512,512]{2,1,0:T(8,128)}, s32[]{:T(128)}, s32[]{:T(128)}) while((s32[]{:T(128)}, f32[4,512,32]{1,2,0:T(8,128)S(1)}, f32[512,32]{0,1:T(8,128)S(1)}, s32[]{:T(128)}, ...), condition=%wide.region_13.14_spmd.clone, body=%wide.region_8.13_spmd.clone.sunk | while | flops 100810760 | bytes 2884979 | solution.py:79
  157.7 1.9 collective-permute-start
  159.8 5.4 %collective-permute-done = f32[512,32]{0,1:T(8,128)S(1)} collective-permute-done((f32[512,32]{0,1:T(8,128)S(1)}, f32[512,32]{0,1:T(8,128)S(1)}, u32[]{:S(2)}, u32[]{:S(2)}) %collective-permute-start) | collective-permute-done | bytes 65568 | tf_op jit(solution)/shard_map/while/body/eval_jaxpr/ppermute | solution.py:23
  165.9 2.2 collective-permute-start
  168.2 13.4 %collective-permute-done = f32[512,32]{0,1:T(8,128)S(1)} collective-permute-done((f32[512,32]{0,1:T(8,128)S(1)}, f32[512,32]{0,1:T(8,128)S(1)}, u32[]{:S(2)}, u32[]{:S(2)}) %collective-permute-start) | collective-permute-done | bytes 65568 | tf_op jit(solution)/shard_map/while/body/eval_jaxpr/ppermute | solution.py:23
  182.4 1.9 collective-permute-start
  184.4 5.0 %collective-permute-done = f32[512,32]{0,1:T(8,128)S(1)} collective-permute-done((f32[512,32]{0,1:T(8,128)S(1)}, f32[512,32]{0,1:T(8,128)S(1)}, u32[]{:S(2)}, u32[]{:S(2)}) %collective-permute-start) | collective-permute-done | bytes 65568 | tf_op jit(solution)/shard_map/while/body/eval_jaxpr/ppermute | solution.py:23
  190.1 1.9 collective-permute-start
  192.2 11.9 %collective-permute-done = f32[512,32]{0,1:T(8,128)S(1)} collective-permute-done((f32[512,32]{0,1:T(8,128)S(1)}, f32[512,32]{0,1:T(8,128)S(1)}, u32[]{:S(2)}, u32[]{:S(2)}) %collective-permute-start) | collective-permute-done | bytes 65568 | tf_op jit(solution)/shard_map/while/body/eval_jaxpr/ppermute | solution.py:23
  204.8 1.9 collective-permute-start
  206.9 62.3 %collective-permute-done = f32[512,32]{0,1:T(8,128)S(1)} collective-permute-done((f32[512,32]{0,1:T(8,128)S(1)}, f32[512,32]{0,1:T(8,128)S(1)}, u32[]{:S(2)}, u32[]{:S(2)}) %collective-permute-start) | collective-permute-done | bytes 65568 | tf_op jit(solution)/shard_map/while/body/eval_jaxpr/ppermute | solution.py:23
  269.2 12.4 %conditional.7 = (f32[512,32]{0,1:T(8,128)S(1)}, f32[4,512,32]{1,2,0:T(8,128)}) conditional(s32[]{:T(128)} %convert_element_type.27, () %tuple.153, (f32[4,512,32]{1,2,0:T(8,128)S(1)}, f32[4,512,512]{2,1,0:T(8,128)}, f32[512,32]{0,1:T(8,128)S(1)}) %tuple.154), branch_computations={%region_9.9_spmd, %region_10.12_spmd} | conditional | flops 100679680 | bytes 1836205 | solution.py:74
  270.0 11.7 %while.59 = (s32[]{:T(128)}, f32[512,32]{0,1:T(8,128)S(1)}, f32[4,512,32]{1,2,0:T(8,128)}, f32[4,512,32]{1,2,0:T(8,128)S(1)}, f32[4,512,512]{2,1,0:T(8,128)}, /*index=5*/s32[]{:T(128)}, s32[]{:T(128)}) while((s32[]{:T(128)}, f32[512,32]{0,1:T(8,128)S(1)}, f32[4,512,32]{1,2,0:T(8,128)}, f32[4,512,32]{1,2,0:T(8,128)S(1)}, ...), condition=%wide.region_12.11_spmd, body=%wide.region_11.10_spmd.sunk | while | flops 100679680 | bytes 1442905 | solution.py:53
  270.0 2.9 bitcast_dynamic-update-slice_fusion.4
  272.9 2.9 bitcast_dynamic-update-slice_fusion.4
  275.8 2.9 bitcast_dynamic-update-slice_fusion.4
  278.7 2.9 bitcast_dynamic-update-slice_fusion.4
  281.7 1.9 collective-permute-start
  284.6 3.2 collective-permute-done
  288.5 14.5 %collective-permute-start = (f32[512,32]{0,1:T(8,128)S(1)}, f32[512,32]{0,1:T(8,128)S(1)}, u32[]{:S(2)}, u32[]{:S(2)}) collective-permute-start(f32[512,32]{0,1:T(8,128)S(1)} %get-tuple-element.651), channel_id=1, source_target_pairs={{4,0},{8,4},{12,8},{16,12},{20,16},{24,20},{28,24},{5,1},{9,5},{13... | collective-permute-start | bytes 196616 | tf_op jit(solution)/shard_map/while/body/eval_jaxpr/ppermute | solution.py:23
  305.7 5.2 %collective-permute-start = (f32[512,32]{0,1:T(8,128)S(1)}, f32[512,32]{0,1:T(8,128)S(1)}, u32[]{:S(2)}, u32[]{:S(2)}) collective-permute-start(f32[512,32]{0,1:T(8,128)S(1)} %get-tuple-element.651), channel_id=1, source_target_pairs={{4,0},{8,4},{12,8},{16,12},{20,16},{24,20},{28,24},{5,1},{9,5},{13... | collective-permute-start | bytes 196616 | tf_op jit(solution)/shard_map/while/body/eval_jaxpr/ppermute | solution.py:23
  314.5 5.1 %all-to-all-start.1 = ((f32[4,1,16384]{2,1,0:T(1,128)}), f32[4,1,16384]{2,1,0:T(1,128)S(1)}, u32[]{:S(2)}, u32[]{:S(2)}) async-start(f32[4,1,16384]{2,1,0:T(1,128)} %reshape.6), calls=%async_computation.1 | async-start | bytes 524288 | tf_op jit(solution)/shard_map/all_to_all | solution.py:103
  319.6 4.3 all-to-all-done.1
  326.8 12.7 %collective-permute-start.2 = (f32[1,128,128]{1,2,0:T(8,128)S(1)}, f32[1,128,128]{1,2,0:T(8,128)S(1)}, u32[]{:S(2)}, u32[]{:S(2)}) collective-permute-start(f32[1,128,128]{1,2,0:T(8,128)S(1)} %bitcast.60), channel_id=1, source_target_pairs={{4,0},{8,4},{12,8},{16,12},{20,16},{24,20},{28,24},{5,1},{9,5},{13... | collective-permute-start | bytes 196616 | tf_op jit(solution)/shard_map/ppermute | solution.py:15
  339.5 1.9 collective-permute-start.3
  341.8 4.7 %collective-permute-done.3 = f32[1,128,128]{1,2,0:T(8,128)S(1)} collective-permute-done((f32[1,128,128]{1,2,0:T(8,128)S(1)}, f32[1,128,128]{1,2,0:T(8,128)S(1)}, u32[]{:S(2)}, u32[]{:S(2)}) %collective-permute-start.3) | collective-permute-done | bytes 65568 | tf_op jit(solution)/shard_map/ppermute | solution.py:14
  346.8 1.9 collective-permute-start.4
  348.7 2.4 collective-permute-start.5
  351.2 2.8 collective-permute-done.4
  354.0 3.8 collective-permute-done.5
  358.1 3.4 collective-permute-start.10
  361.5 2.5 collective-permute-start.11
  364.1 1.9 collective-permute-start.8
  366.1 2.4 collective-permute-start.9
  368.8 3.1 collective-permute-start.12
  371.9 1.9 collective-permute-start.13
  375.2 2.0 collective-permute-done.12
  377.2 3.8 collective-permute-done.13
  383.4 41.7 %all-reduce.6 = (f32[]{:T(128)}, f32[]{:T(128)}, f32[]{:T(128)}, f32[]{:T(128)}, f32[]{:T(128)}, /*index=5*/f32[]{:T(128)}, f32[]{:T(128)}, f32[]{:T(128)}) all-reduce(f32[]{:T(128)} %get-tuple-element.434, f32[]{:T(128)} %multiply_reduce_fusion.8, f32[]{:T(128)} %get-tuple-element.433, ...), channel_id=1, replica_groups=mesh['layer'=8,'split'=4] {'layer','split'}, use_global_device_ids=true, to_apply=%region_17.18 | all-reduce | flops 8 | bytes 64 | tf_op jit(solution)/shard_map/psum | solution.py:106
  (120 shorter events, 48.6 us)
Async XLA Ops:
  7.2 37.6 %all-gather.2.cloned.1.call-start = ((), (), s32[]{:S(2)}) async-start(), calls=%async_computation.2 | async-start | bytes 5242880 | tf_op jit(solution)/shard_map/all_gather | solution.py:86
  9.7 13.7 %all-to-all-start = ((f32[4,128,128]{1,0,2:T(4,128)}), f32[4,128,128]{1,0,2:T(4,128)S(1)}, u32[]{:S(2)}, u32[]{:S(2)}) async-start(f32[4,128,128]{1,0,2:T(4,128)} %copy.44), calls=%async_computation | async-start | bytes 524288 | tf_op jit(solution)/shard_map/all_to_all | solution.py:87
  14.7 326.8 %collective-permute-start.6 = (f32[1,128,128]{1,2,0:T(8,128)S(1)}, f32[1,128,128]{1,2,0:T(8,128)S(1)}, u32[]{:S(2)}, u32[]{:S(2)}) collective-permute-start(f32[1,128,128]{1,2,0:T(8,128)S(1)} %get-tuple-element.507), channel_id=1, source_target_pairs={{4,0},{8,4},{12,8},{16,12},{20,16},{24,20},{28,24},{5,1},{9,5},{13... | collective-permute-start | bytes 196616 | tf_op jit(solution)/shard_map/ppermute | solution.py:15
  18.0 323.5 %collective-permute-start.7 = (f32[1,128,128]{1,2,0:T(8,128)S(1)}, f32[1,128,128]{1,2,0:T(8,128)S(1)}, u32[]{:S(2)}, u32[]{:S(2)}) collective-permute-start(f32[1,128,128]{1,2,0:T(8,128)S(1)} %get-tuple-element.506), channel_id=1, source_target_pairs={{0,4},{4,8},{8,12},{12,16},{16,20},{20,24},{24,28},{1,5},{5,9},{9,... | collective-permute-start | bytes 196616 | tf_op jit(solution)/shard_map/ppermute | solution.py:14
  45.5 7.0 %collective-permute-start.1 = (f32[512,32]{0,1:T(8,128)S(1)}, f32[512,32]{0,1:T(8,128)S(1)}, u32[]{:S(2)}, u32[]{:S(2)}) collective-permute-start(f32[512,32]{0,1:T(8,128)S(1)} %get-tuple-element.643), channel_id=1, source_target_pairs={{0,4},{4,8},{8,12},{12,16},{16,20},{20,24},{24,28},{1,5},{5,9},{9,... | collective-permute-start | bytes 196616 | tf_op jit(solution)/shard_map/while/body/eval_jaxpr/ppermute | solution.py:23
  53.3 24.6 %collective-permute-start.1 = (f32[512,32]{0,1:T(8,128)S(1)}, f32[512,32]{0,1:T(8,128)S(1)}, u32[]{:S(2)}, u32[]{:S(2)}) collective-permute-start(f32[512,32]{0,1:T(8,128)S(1)} %get-tuple-element.643), channel_id=1, source_target_pairs={{0,4},{4,8},{8,12},{12,16},{16,20},{20,24},{24,28},{1,5},{5,9},{9,... | collective-permute-start | bytes 196616 | tf_op jit(solution)/shard_map/while/body/eval_jaxpr/ppermute | solution.py:23
  89.6 7.1 %collective-permute-start.1 = (f32[512,32]{0,1:T(8,128)S(1)}, f32[512,32]{0,1:T(8,128)S(1)}, u32[]{:S(2)}, u32[]{:S(2)}) collective-permute-start(f32[512,32]{0,1:T(8,128)S(1)} %get-tuple-element.643), channel_id=1, source_target_pairs={{0,4},{4,8},{8,12},{12,16},{16,20},{20,24},{24,28},{1,5},{5,9},{9,... | collective-permute-start | bytes 196616 | tf_op jit(solution)/shard_map/while/body/eval_jaxpr/ppermute | solution.py:23
  97.4 13.9 %collective-permute-start.1 = (f32[512,32]{0,1:T(8,128)S(1)}, f32[512,32]{0,1:T(8,128)S(1)}, u32[]{:S(2)}, u32[]{:S(2)}) collective-permute-start(f32[512,32]{0,1:T(8,128)S(1)} %get-tuple-element.643), channel_id=1, source_target_pairs={{0,4},{4,8},{8,12},{12,16},{16,20},{20,24},{24,28},{1,5},{5,9},{9,... | collective-permute-start | bytes 196616 | tf_op jit(solution)/shard_map/while/body/eval_jaxpr/ppermute | solution.py:23
  112.0 7.0 %collective-permute-start.1 = (f32[512,32]{0,1:T(8,128)S(1)}, f32[512,32]{0,1:T(8,128)S(1)}, u32[]{:S(2)}, u32[]{:S(2)}) collective-permute-start(f32[512,32]{0,1:T(8,128)S(1)} %get-tuple-element.643), channel_id=1, source_target_pairs={{0,4},{4,8},{8,12},{12,16},{16,20},{20,24},{24,28},{1,5},{5,9},{9,... | collective-permute-start | bytes 196616 | tf_op jit(solution)/shard_map/while/body/eval_jaxpr/ppermute | solution.py:23
  119.8 14.8 %collective-permute-start.1 = (f32[512,32]{0,1:T(8,128)S(1)}, f32[512,32]{0,1:T(8,128)S(1)}, u32[]{:S(2)}, u32[]{:S(2)}) collective-permute-start(f32[512,32]{0,1:T(8,128)S(1)} %get-tuple-element.643), channel_id=1, source_target_pairs={{0,4},{4,8},{8,12},{12,16},{16,20},{20,24},{24,28},{1,5},{5,9},{9,... | collective-permute-start | bytes 196616 | tf_op jit(solution)/shard_map/while/body/eval_jaxpr/ppermute | solution.py:23
  135.3 7.0 %collective-permute-start.1 = (f32[512,32]{0,1:T(8,128)S(1)}, f32[512,32]{0,1:T(8,128)S(1)}, u32[]{:S(2)}, u32[]{:S(2)}) collective-permute-start(f32[512,32]{0,1:T(8,128)S(1)} %get-tuple-element.643), channel_id=1, source_target_pairs={{0,4},{4,8},{8,12},{12,16},{16,20},{20,24},{24,28},{1,5},{5,9},{9,... | collective-permute-start | bytes 196616 | tf_op jit(solution)/shard_map/while/body/eval_jaxpr/ppermute | solution.py:23
  143.1 13.9 %collective-permute-start.1 = (f32[512,32]{0,1:T(8,128)S(1)}, f32[512,32]{0,1:T(8,128)S(1)}, u32[]{:S(2)}, u32[]{:S(2)}) collective-permute-start(f32[512,32]{0,1:T(8,128)S(1)} %get-tuple-element.643), channel_id=1, source_target_pairs={{0,4},{4,8},{8,12},{12,16},{16,20},{20,24},{24,28},{1,5},{5,9},{9,... | collective-permute-start | bytes 196616 | tf_op jit(solution)/shard_map/while/body/eval_jaxpr/ppermute | solution.py:23
  157.7 7.4 %collective-permute-start = (f32[512,32]{0,1:T(8,128)S(1)}, f32[512,32]{0,1:T(8,128)S(1)}, u32[]{:S(2)}, u32[]{:S(2)}) collective-permute-start(f32[512,32]{0,1:T(8,128)S(1)} %get-tuple-element.651), channel_id=1, source_target_pairs={{4,0},{8,4},{12,8},{16,12},{20,16},{24,20},{28,24},{5,1},{9,5},{13... | collective-permute-start | bytes 196616 | tf_op jit(solution)/shard_map/while/body/eval_jaxpr/ppermute | solution.py:23
  165.9 15.7 %collective-permute-start = (f32[512,32]{0,1:T(8,128)S(1)}, f32[512,32]{0,1:T(8,128)S(1)}, u32[]{:S(2)}, u32[]{:S(2)}) collective-permute-start(f32[512,32]{0,1:T(8,128)S(1)} %get-tuple-element.651), channel_id=1, source_target_pairs={{4,0},{8,4},{12,8},{16,12},{20,16},{24,20},{28,24},{5,1},{9,5},{13... | collective-permute-start | bytes 196616 | tf_op jit(solution)/shard_map/while/body/eval_jaxpr/ppermute | solution.py:23
  182.4 7.0 %collective-permute-start = (f32[512,32]{0,1:T(8,128)S(1)}, f32[512,32]{0,1:T(8,128)S(1)}, u32[]{:S(2)}, u32[]{:S(2)}) collective-permute-start(f32[512,32]{0,1:T(8,128)S(1)} %get-tuple-element.651), channel_id=1, source_target_pairs={{4,0},{8,4},{12,8},{16,12},{20,16},{24,20},{28,24},{5,1},{9,5},{13... | collective-permute-start | bytes 196616 | tf_op jit(solution)/shard_map/while/body/eval_jaxpr/ppermute | solution.py:23
  190.1 14.0 %collective-permute-start = (f32[512,32]{0,1:T(8,128)S(1)}, f32[512,32]{0,1:T(8,128)S(1)}, u32[]{:S(2)}, u32[]{:S(2)}) collective-permute-start(f32[512,32]{0,1:T(8,128)S(1)} %get-tuple-element.651), channel_id=1, source_target_pairs={{4,0},{8,4},{12,8},{16,12},{20,16},{24,20},{28,24},{5,1},{9,5},{13... | collective-permute-start | bytes 196616 | tf_op jit(solution)/shard_map/while/body/eval_jaxpr/ppermute | solution.py:23
  204.8 64.4 %collective-permute-start = (f32[512,32]{0,1:T(8,128)S(1)}, f32[512,32]{0,1:T(8,128)S(1)}, u32[]{:S(2)}, u32[]{:S(2)}) collective-permute-start(f32[512,32]{0,1:T(8,128)S(1)} %get-tuple-element.651), channel_id=1, source_target_pairs={{4,0},{8,4},{12,8},{16,12},{20,16},{24,20},{28,24},{5,1},{9,5},{13... | collective-permute-start | bytes 196616 | tf_op jit(solution)/shard_map/while/body/eval_jaxpr/ppermute | solution.py:23
  281.7 6.2 %collective-permute-start = (f32[512,32]{0,1:T(8,128)S(1)}, f32[512,32]{0,1:T(8,128)S(1)}, u32[]{:S(2)}, u32[]{:S(2)}) collective-permute-start(f32[512,32]{0,1:T(8,128)S(1)} %get-tuple-element.651), channel_id=1, source_target_pairs={{4,0},{8,4},{12,8},{16,12},{20,16},{24,20},{28,24},{5,1},{9,5},{13... | collective-permute-start | bytes 196616 | tf_op jit(solution)/shard_map/while/body/eval_jaxpr/ppermute | solution.py:23
  288.5 16.4 %collective-permute-start = (f32[512,32]{0,1:T(8,128)S(1)}, f32[512,32]{0,1:T(8,128)S(1)}, u32[]{:S(2)}, u32[]{:S(2)}) collective-permute-start(f32[512,32]{0,1:T(8,128)S(1)} %get-tuple-element.651), channel_id=1, source_target_pairs={{4,0},{8,4},{12,8},{16,12},{20,16},{24,20},{28,24},{5,1},{9,5},{13... | collective-permute-start | bytes 196616 | tf_op jit(solution)/shard_map/while/body/eval_jaxpr/ppermute | solution.py:23
  305.7 7.0 %collective-permute-start = (f32[512,32]{0,1:T(8,128)S(1)}, f32[512,32]{0,1:T(8,128)S(1)}, u32[]{:S(2)}, u32[]{:S(2)}) collective-permute-start(f32[512,32]{0,1:T(8,128)S(1)} %get-tuple-element.651), channel_id=1, source_target_pairs={{4,0},{8,4},{12,8},{16,12},{20,16},{24,20},{28,24},{5,1},{9,5},{13... | collective-permute-start | bytes 196616 | tf_op jit(solution)/shard_map/while/body/eval_jaxpr/ppermute | solution.py:23
  314.5 9.4 %all-to-all-start.1 = ((f32[4,1,16384]{2,1,0:T(1,128)}), f32[4,1,16384]{2,1,0:T(1,128)S(1)}, u32[]{:S(2)}, u32[]{:S(2)}) async-start(f32[4,1,16384]{2,1,0:T(1,128)} %reshape.6), calls=%async_computation.1 | async-start | bytes 524288 | tf_op jit(solution)/shard_map/all_to_all | solution.py:103
  326.8 15.1 %collective-permute-start.2 = (f32[1,128,128]{1,2,0:T(8,128)S(1)}, f32[1,128,128]{1,2,0:T(8,128)S(1)}, u32[]{:S(2)}, u32[]{:S(2)}) collective-permute-start(f32[1,128,128]{1,2,0:T(8,128)S(1)} %bitcast.60), channel_id=1, source_target_pairs={{4,0},{8,4},{12,8},{16,12},{20,16},{24,20},{28,24},{5,1},{9,5},{13... | collective-permute-start | bytes 196616 | tf_op jit(solution)/shard_map/ppermute | solution.py:15
  339.5 7.1 %collective-permute-start.3 = (f32[1,128,128]{1,2,0:T(8,128)S(1)}, f32[1,128,128]{1,2,0:T(8,128)S(1)}, u32[]{:S(2)}, u32[]{:S(2)}) collective-permute-start(f32[1,128,128]{1,2,0:T(8,128)S(1)} %bitcast.61), channel_id=1, source_target_pairs={{0,4},{4,8},{8,12},{12,16},{16,20},{20,24},{24,28},{1,5},{5,9},{9,... | collective-permute-start | bytes 196616 | tf_op jit(solution)/shard_map/ppermute | solution.py:14
  346.8 7.2 %collective-permute-start.4 = (f32[6,1,128]{1,2,0:T(8,128)S(1)}, f32[6,1,128]{1,2,0:T(8,128)S(1)}, u32[]{:S(2)}, u32[]{:S(2)}) collective-permute-start(f32[6,1,128]{1,2,0:T(8,128)S(1)} %get-tuple-element.500), channel_id=1, source_target_pairs={{1,0},{2,1},{3,2},{5,4},{6,5},{7,6},{9,8},{10,9},{11,10},{13,12},{... | collective-permute-start | bytes 9224 | tf_op jit(solution)/shard_map/ppermute | solution.py:15
  348.7 9.1 %collective-permute-start.5 = (f32[6,1,128]{1,2,0:T(8,128)S(1)}, f32[6,1,128]{1,2,0:T(8,128)S(1)}, u32[]{:S(2)}, u32[]{:S(2)}) collective-permute-start(f32[6,1,128]{1,2,0:T(8,128)S(1)} %get-tuple-element.501), channel_id=1, source_target_pairs={{0,1},{1,2},{2,3},{4,5},{5,6},{6,7},{8,9},{9,10},{10,11},{12,13},{... | collective-permute-start | bytes 9224 | tf_op jit(solution)/shard_map/ppermute | solution.py:14
  358.1 10.4 %collective-permute-start.10 = (f32[1,128,128]{1,2,0:T(8,128)S(1)}, f32[1,128,128]{1,2,0:T(8,128)S(1)}, u32[]{:S(2)}, u32[]{:S(2)}) collective-permute-start(f32[1,128,128]{1,2,0:T(8,128)S(1)} %get-tuple-element.503), channel_id=1, source_target_pairs={{4,0},{8,4},{12,8},{16,12},{20,16},{24,20},{28,24},{5,1},{9,5},{13... | collective-permute-start | bytes 196616 | tf_op jit(solution)/shard_map/ppermute | solution.py:15
  361.5 7.1 %collective-permute-start.11 = (f32[1,128,128]{1,2,0:T(8,128)S(1)}, f32[1,128,128]{1,2,0:T(8,128)S(1)}, u32[]{:S(2)}, u32[]{:S(2)}) collective-permute-start(f32[1,128,128]{1,2,0:T(8,128)S(1)} %get-tuple-element.502), channel_id=1, source_target_pairs={{0,4},{4,8},{8,12},{12,16},{16,20},{20,24},{24,28},{1,5},{5,9},{9,... | collective-permute-start | bytes 196616 | tf_op jit(solution)/shard_map/ppermute | solution.py:14
  364.1 9.7 %collective-permute-start.8 = (f32[6,1,128]{1,2,0:T(8,128)S(1)}, f32[6,1,128]{1,2,0:T(8,128)S(1)}, u32[]{:S(2)}, u32[]{:S(2)}) collective-permute-start(f32[6,1,128]{1,2,0:T(8,128)S(1)} %get-tuple-element.498), channel_id=1, source_target_pairs={{1,0},{2,1},{3,2},{5,4},{6,5},{7,6},{9,8},{10,9},{11,10},{13,12},{... | collective-permute-start | bytes 9224 | tf_op jit(solution)/shard_map/ppermute | solution.py:15
  366.1 9.1 %collective-permute-start.9 = (f32[6,1,128]{1,2,0:T(8,128)S(1)}, f32[6,1,128]{1,2,0:T(8,128)S(1)}, u32[]{:S(2)}, u32[]{:S(2)}) collective-permute-start(f32[6,1,128]{1,2,0:T(8,128)S(1)} %get-tuple-element.499), channel_id=1, source_target_pairs={{0,1},{1,2},{2,3},{4,5},{5,6},{6,7},{8,9},{9,10},{10,11},{12,13},{... | collective-permute-start | bytes 9224 | tf_op jit(solution)/shard_map/ppermute | solution.py:14
  368.8 8.4 %collective-permute-start.12 = (f32[6,1,128]{1,2,0:T(8,128)S(1)}, f32[6,1,128]{1,2,0:T(8,128)S(1)}, u32[]{:S(2)}, u32[]{:S(2)}) collective-permute-start(f32[6,1,128]{1,2,0:T(8,128)S(1)} %get-tuple-element.496), channel_id=1, source_target_pairs={{1,0},{2,1},{3,2},{5,4},{6,5},{7,6},{9,8},{10,9},{11,10},{13,12},{... | collective-permute-start | bytes 9224 | tf_op jit(solution)/shard_map/ppermute | solution.py:15
  371.9 9.1 %collective-permute-start.13 = (f32[6,1,128]{1,2,0:T(8,128)S(1)}, f32[6,1,128]{1,2,0:T(8,128)S(1)}, u32[]{:S(2)}, u32[]{:S(2)}) collective-permute-start(f32[6,1,128]{1,2,0:T(8,128)S(1)} %get-tuple-element.497), channel_id=1, source_target_pairs={{0,1},{1,2},{2,3},{4,5},{5,6},{6,7},{8,9},{9,10},{10,11},{12,13},{... | collective-permute-start | bytes 9224 | tf_op jit(solution)/shard_map/ppermute | solution.py:14
Sparse Core Ops, SparseCore 0:
  9.5 35.1 all-gather.1
where the time goes:
time: 441 us; the launch traced here: 439 us
  waiting for transfers between devices  189 us (43%)
  starting transfers between devices  134 us (30%)
  blocking collectives  41.7 us (9%)
  matrix products  23.3 us (5%)
  local copies, waits for them, and re-layouts  20.9 us (5%)
  between operations  20.8 us (5%)
  other arithmetic  8.15 us (2%)
    ppermute x16, waiting for transfers between devices, from_behind(): return lax.ppermute(block, axis, route)  144 us
    ppermute x16, starting transfers between devices, from_behind(): return lax.ppermute(block, axis, route)  85.4 us
    psum x1, blocking collectives, per_device(): lax.psum((jnp.sum(right_side * right_side), jnp.sum(right_side * image),...  41.7 us
    ppermute x6, starting transfers between devices, with_halo(): after = lax.ppermute(first, axis, down)  26.3 us
    all_gather x1, waiting for transfers between devices, per_device(): matrices = lax.all_gather(inverses, 'split', axis=2, tiled=True)  21.4 us
    ppermute x6, starting transfers between devices, with_halo(): before = lax.ppermute(last, axis, up)  13.7 us
    ppermute x6, waiting for transfers between devices, with_halo(): before = lax.ppermute(last, axis, up)  13.7 us
    dot_general x4, matrix products, down_advance(): state = jnp.dot(matrix, source + state, precision=lax.Precision.HIGHEST)  11.7 us
  transfers between devices with their start and end apart: 31, of which 24 were waited for; matrix products, arithmetic and copies ran while one was open for 11% of the time, Pallas kernels for 0%

commit v1 on v0

--- a/solution.py
+++ b/solution.py
@@ -2,6 +2,7 @@
 import jax.numpy as jnp
 from jax import lax
 from jax.sharding import PartitionSpec as P
+from jax.lax import psum
 
 
 def with_halo(x, sides, width):
@@ -103,20 +104,19 @@
     direction = lax.all_to_all(upper_sweep, "split", split_axis=1, concat_axis=2, tiled=True)
     image = stencil(direction, diagonal)
     applied_image = stencil(image, diagonal)
-    sums_all = lax.psum(
-        (
-            jnp.sum(right_side * right_side),
-            jnp.sum(right_side * image),
-            jnp.sum(applied_rhs * right_side),
-            jnp.sum(applied_rhs * image),
-            jnp.sum(applied_image * right_side),
-            jnp.sum(applied_image * image),
-            jnp.sum(applied_rhs * applied_rhs),
-            jnp.sum(applied_rhs * applied_image),
-            jnp.sum(applied_image * applied_image),
-        ),
-        ("layer", "split"),
+    sums_all = (
+        jnp.sum(right_side * right_side),
+        jnp.sum(right_side * image),
+        jnp.sum(applied_rhs * right_side),
+        jnp.sum(applied_rhs * image),
+        jnp.sum(applied_image * right_side),
+        jnp.sum(applied_image * image),
+        jnp.sum(applied_rhs * applied_rhs),
+        jnp.sum(applied_rhs * applied_image),
+        jnp.sum(applied_image * applied_image),
     )
+    for no in ("split", "layer"):
+        sums_all = psum(sums_all, axis_name=no)
     (
         norm_sq,
         curv_sum,

time: 441 us -> 426 us (0.966)
  blocking collectives: 41.7 us -> 24 us
    psum x1 -> x2, blocking collectives: 41.7 us -> 24 us  [per_device(): sums_all = psum(sums_all, axis_name=no)]
  transfers between devices with their start and end apart: 31 -> 31, of which waited for: 24 -> 24; matrix products, arithmetic and copies ran while one was open for 11% -> 12% of each run, Pallas kernels for 0% -> 0%
where the time goes in v1:
time: 426 us; the launch traced here: 421 us
  waiting for transfers between devices  189 us (44%)
  starting transfers between devices  134 us (31%)
  blocking collectives  24 us (6%)
  matrix products  23.3 us (5%)
  local copies, waits for them, and re-layouts  20.9 us (5%)
  between operations  20.7 us (5%)
  other arithmetic  8.09 us (2%)
    ppermute x16, waiting for transfers between devices, from_behind(): return lax.ppermute(block, axis, route)  144 us
    ppermute x16, starting transfers between devices, from_behind(): return lax.ppermute(block, axis, route)  85.4 us
    ppermute x6, starting transfers between devices, with_halo(): after = lax.ppermute(first, axis, down)  26.3 us
    psum x2, blocking collectives, per_device(): sums_all = psum(sums_all, axis_name=no)  24 us
    all_gather x1, waiting for transfers between devices, per_device(): matrices = lax.all_gather(inverses, 'split', axis=2, tiled=True)  21.4 us
    ppermute x6, starting transfers between devices, with_halo(): before = lax.ppermute(last, axis, up)  13.7 us
    ppermute x6, waiting for transfers between devices, with_halo(): before = lax.ppermute(last, axis, up)  13.7 us
    dot_general x4, matrix products, down_advance(): state = jnp.dot(matrix, source + state, precision=lax.Precision.HIGHEST)  11.7 us
  transfers between devices with their start and end apart: 31, of which 24 were waited for; matrix products, arithmetic and copies ran while one was open for 12% of the time, Pallas kernels for 0%

profile of v1, /device:TPU:12, one launch (start us, length us, event | category | flops | bytes accessed | tf_op | source)
XLA Modules:
  0.0 421.2 jit_solution(15041742059451401053)
XLA Ops:
  7.9 1.8 copy.44
  9.7 3.9 all-to-all-start
  14.7 3.3 collective-permute-start.6
  18.0 2.6 collective-permute-start.7
  23.3 21.4 %all-gather.2.cloned.1.call-done = f32[4,512,512]{2,1,0:T(8,128)} async-done(((f32[4,512,128]{2,1,0:T(8,128)}), f32[4,512,512]{2,1,0:T(8,128)}) %all-gather.2.cloned.1.call-update) | async-done | bytes 4194320 | tf_op jit(solution)/shard_map/all_gather | solution.py:87
  44.8 112.2 %while.60 = (s32[]{:T(128)}, f32[4,512,32]{1,2,0:T(8,128)S(1)}, f32[512,32]{0,1:T(8,128)S(1)}, s32[]{:T(128)}, f32[4,512,512]{2,1,0:T(8,128)}, /*index=5*/f32[4,512,32]{1,2,0:T(8,128)S(1)}, s32[]{:T(128)}, s32[]{:T(128)}) while((s32[]{:T(128)}, f32[4,512,32]{1,2,0:T(8,128)S(1)}, f32[512,32]{0,1:T(8,128)S(1)}, s32[]{:T(128)}, ...), condition=%wide.region_8.9_spmd.clone, body=%wide.region_3.8_spmd.clone.sunk | while | flops 100810760 | bytes 2623315 | solution.py:80
  45.5 3.4 collective-permute-start.1
  49.0 3.6 collective-permute-done.1
  53.3 2.5 collective-permute-start.1
  55.9 22.0 %collective-permute-done.1 = f32[512,32]{0,1:T(8,128)S(1)} collective-permute-done((f32[512,32]{0,1:T(8,128)S(1)}, f32[512,32]{0,1:T(8,128)S(1)}, u32[]{:S(2)}, u32[]{:S(2)}) %collective-permute-start.1) | collective-permute-done | bytes 65568 | tf_op jit(solution)/shard_map/while/body/eval_jaxpr/ppermute | solution.py:24
  77.9 11.7 %conditional.6 = (f32[512,32]{0,1:T(8,128)S(1)}, f32[4,512,32]{1,2,0:T(8,128)}) conditional(s32[]{:T(128)} %convert_element_type.26, () %tuple.150, (f32[4,512,512]{2,1,0:T(8,128)}, f32[4,512,32]{1,2,0:T(8,128)S(1)}, f32[512,32]{0,1:T(8,128)S(1)}) %tuple.151), branch_computations={%region_4.4_spmd, %region_5.7_spmd} | conditional | flops 100679680 | bytes 1574541 | solution.py:75
  77.9 11.7 %while.58 = (s32[]{:T(128)}, f32[512,32]{0,1:T(8,128)S(1)}, f32[4,512,32]{1,2,0:T(8,128)}, f32[4,512,512]{2,1,0:T(8,128)}, f32[4,512,32]{1,2,0:T(8,128)S(1)}, /*index=5*/s32[]{:T(128)}) while((s32[]{:T(128)}, f32[512,32]{0,1:T(8,128)S(1)}, f32[4,512,32]{1,2,0:T(8,128)}, f32[4,512,512]{2,1,0:T(8,128)}, f32[4,512,32]{1,2,0:T(8,128)S(1)}, ...), condition=%wide.region_7.6_spmd, body=%wide.region_6.5_spmd.sunk | while | flops 100679680 | bytes 1443397 | solution.py:44
  77.9 2.9 bitcast_dynamic-update-slice_fusion.5
  80.8 2.9 bitcast_dynamic-update-slice_fusion.5
  83.8 2.9 bitcast_dynamic-update-slice_fusion.5
  86.7 2.9 bitcast_dynamic-update-slice_fusion.5
  89.6 1.9 collective-permute-start.1
  92.6 4.1 collective-permute-done.1
  97.4 12.0 %collective-permute-start.1 = (f32[512,32]{0,1:T(8,128)S(1)}, f32[512,32]{0,1:T(8,128)S(1)}, u32[]{:S(2)}, u32[]{:S(2)}) collective-permute-start(f32[512,32]{0,1:T(8,128)S(1)} %get-tuple-element.651), channel_id=1, source_target_pairs={{0,4},{4,8},{8,12},{12,16},{16,20},{20,24},{24,28},{1,5},{5,9},{9,... | collective-permute-start | bytes 196616 | tf_op jit(solution)/shard_map/while/body/eval_jaxpr/ppermute | solution.py:24
  112.0 4.3 %collective-permute-start.1 = (f32[512,32]{0,1:T(8,128)S(1)}, f32[512,32]{0,1:T(8,128)S(1)}, u32[]{:S(2)}, u32[]{:S(2)}) collective-permute-start(f32[512,32]{0,1:T(8,128)S(1)} %get-tuple-element.651), channel_id=1, source_target_pairs={{0,4},{4,8},{8,12},{12,16},{16,20},{20,24},{24,28},{1,5},{5,9},{9,... | collective-permute-start | bytes 196616 | tf_op jit(solution)/shard_map/while/body/eval_jaxpr/ppermute | solution.py:24
  116.4 2.7 collective-permute-done.1
  119.8 12.9 %collective-permute-start.1 = (f32[512,32]{0,1:T(8,128)S(1)}, f32[512,32]{0,1:T(8,128)S(1)}, u32[]{:S(2)}, u32[]{:S(2)}) collective-permute-start(f32[512,32]{0,1:T(8,128)S(1)} %get-tuple-element.651), channel_id=1, source_target_pairs={{0,4},{4,8},{8,12},{12,16},{16,20},{20,24},{24,28},{1,5},{5,9},{9,... | collective-permute-start | bytes 196616 | tf_op jit(solution)/shard_map/while/body/eval_jaxpr/ppermute | solution.py:24
  135.3 5.2 %collective-permute-start.1 = (f32[512,32]{0,1:T(8,128)S(1)}, f32[512,32]{0,1:T(8,128)S(1)}, u32[]{:S(2)}, u32[]{:S(2)}) collective-permute-start(f32[512,32]{0,1:T(8,128)S(1)} %get-tuple-element.651), channel_id=1, source_target_pairs={{0,4},{4,8},{8,12},{12,16},{16,20},{20,24},{24,28},{1,5},{5,9},{9,... | collective-permute-start | bytes 196616 | tf_op jit(solution)/shard_map/while/body/eval_jaxpr/ppermute | solution.py:24
  143.1 12.0 %collective-permute-start.1 = (f32[512,32]{0,1:T(8,128)S(1)}, f32[512,32]{0,1:T(8,128)S(1)}, u32[]{:S(2)}, u32[]{:S(2)}) collective-permute-start(f32[512,32]{0,1:T(8,128)S(1)} %get-tuple-element.651), channel_id=1, source_target_pairs={{0,4},{4,8},{8,12},{12,16},{16,20},{20,24},{24,28},{1,5},{5,9},{9,... | collective-permute-start | bytes 196616 | tf_op jit(solution)/shard_map/while/body/eval_jaxpr/ppermute | solution.py:24
  157.0 155.7 %while.61 = (s32[]{:T(128)}, f32[4,512,32]{1,2,0:T(8,128)S(1)}, f32[512,32]{0,1:T(8,128)S(1)}, s32[]{:T(128)}, f32[4,512,32]{1,2,0:T(8,128)S(1)}, /*index=5*/f32[4,512,512]{2,1,0:T(8,128)}, s32[]{:T(128)}, s32[]{:T(128)}) while((s32[]{:T(128)}, f32[4,512,32]{1,2,0:T(8,128)S(1)}, f32[512,32]{0,1:T(8,128)S(1)}, s32[]{:T(128)}, ...), condition=%wide.region_14.15_spmd.clone, body=%wide.region_9.0_spmd.clone.sunk | while | flops 100810760 | bytes 2884979 | solution.py:80
  157.7 1.9 collective-permute-start
  159.8 5.4 %collective-permute-done = f32[512,32]{0,1:T(8,128)S(1)} collective-permute-done((f32[512,32]{0,1:T(8,128)S(1)}, f32[512,32]{0,1:T(8,128)S(1)}, u32[]{:S(2)}, u32[]{:S(2)}) %collective-permute-start) | collective-permute-done | bytes 65568 | tf_op jit(solution)/shard_map/while/body/eval_jaxpr/ppermute | solution.py:24
  165.9 2.2 collective-permute-start
  168.2 13.4 %collective-permute-done = f32[512,32]{0,1:T(8,128)S(1)} collective-permute-done((f32[512,32]{0,1:T(8,128)S(1)}, f32[512,32]{0,1:T(8,128)S(1)}, u32[]{:S(2)}, u32[]{:S(2)}) %collective-permute-start) | collective-permute-done | bytes 65568 | tf_op jit(solution)/shard_map/while/body/eval_jaxpr/ppermute | solution.py:24
  182.4 1.9 collective-permute-start
  184.4 5.0 %collective-permute-done = f32[512,32]{0,1:T(8,128)S(1)} collective-permute-done((f32[512,32]{0,1:T(8,128)S(1)}, f32[512,32]{0,1:T(8,128)S(1)}, u32[]{:S(2)}, u32[]{:S(2)}) %collective-permute-start) | collective-permute-done | bytes 65568 | tf_op jit(solution)/shard_map/while/body/eval_jaxpr/ppermute | solution.py:24
  190.1 1.9 collective-permute-start
  192.2 11.9 %collective-permute-done = f32[512,32]{0,1:T(8,128)S(1)} collective-permute-done((f32[512,32]{0,1:T(8,128)S(1)}, f32[512,32]{0,1:T(8,128)S(1)}, u32[]{:S(2)}, u32[]{:S(2)}) %collective-permute-start) | collective-permute-done | bytes 65568 | tf_op jit(solution)/shard_map/while/body/eval_jaxpr/ppermute | solution.py:24
  204.8 1.9 collective-permute-start
  206.9 62.3 %collective-permute-done = f32[512,32]{0,1:T(8,128)S(1)} collective-permute-done((f32[512,32]{0,1:T(8,128)S(1)}, f32[512,32]{0,1:T(8,128)S(1)}, u32[]{:S(2)}, u32[]{:S(2)}) %collective-permute-start) | collective-permute-done | bytes 65568 | tf_op jit(solution)/shard_map/while/body/eval_jaxpr/ppermute | solution.py:24
  269.2 12.4 %conditional.7 = (f32[512,32]{0,1:T(8,128)S(1)}, f32[4,512,32]{1,2,0:T(8,128)}) conditional(s32[]{:T(128)} %convert_element_type.27, () %tuple.153, (f32[4,512,32]{1,2,0:T(8,128)S(1)}, f32[4,512,512]{2,1,0:T(8,128)}, f32[512,32]{0,1:T(8,128)S(1)}) %tuple.154), branch_computations={%region_10.10_spmd, %region_11.13_spmd} | conditional | flops 100679680 | bytes 1836205 | solution.py:75
  270.0 11.7 %while.59 = (s32[]{:T(128)}, f32[512,32]{0,1:T(8,128)S(1)}, f32[4,512,32]{1,2,0:T(8,128)}, f32[4,512,32]{1,2,0:T(8,128)S(1)}, f32[4,512,512]{2,1,0:T(8,128)}, /*index=5*/s32[]{:T(128)}, s32[]{:T(128)}) while((s32[]{:T(128)}, f32[512,32]{0,1:T(8,128)S(1)}, f32[4,512,32]{1,2,0:T(8,128)}, f32[4,512,32]{1,2,0:T(8,128)S(1)}, ...), condition=%wide.region_13.12_spmd, body=%wide.region_12.11_spmd.sunk | while | flops 100679680 | bytes 1442905 | solution.py:54
  270.0 2.9 bitcast_dynamic-update-slice_fusion.4
  272.9 2.9 bitcast_dynamic-update-slice_fusion.4
  275.8 2.9 bitcast_dynamic-update-slice_fusion.4
  278.7 2.9 bitcast_dynamic-update-slice_fusion.4
  281.7 1.9 collective-permute-start
  284.6 3.2 collective-permute-done
  288.5 14.5 %collective-permute-start = (f32[512,32]{0,1:T(8,128)S(1)}, f32[512,32]{0,1:T(8,128)S(1)}, u32[]{:S(2)}, u32[]{:S(2)}) collective-permute-start(f32[512,32]{0,1:T(8,128)S(1)} %get-tuple-element.659), channel_id=1, source_target_pairs={{4,0},{8,4},{12,8},{16,12},{20,16},{24,20},{28,24},{5,1},{9,5},{13... | collective-permute-start | bytes 196616 | tf_op jit(solution)/shard_map/while/body/eval_jaxpr/ppermute | solution.py:24
  305.7 5.2 %collective-permute-start = (f32[512,32]{0,1:T(8,128)S(1)}, f32[512,32]{0,1:T(8,128)S(1)}, u32[]{:S(2)}, u32[]{:S(2)}) collective-permute-start(f32[512,32]{0,1:T(8,128)S(1)} %get-tuple-element.659), channel_id=1, source_target_pairs={{4,0},{8,4},{12,8},{16,12},{20,16},{24,20},{28,24},{5,1},{9,5},{13... | collective-permute-start | bytes 196616 | tf_op jit(solution)/shard_map/while/body/eval_jaxpr/ppermute | solution.py:24
  314.5 5.1 %all-to-all-start.1 = ((f32[4,1,16384]{2,1,0:T(1,128)}), f32[4,1,16384]{2,1,0:T(1,128)S(1)}, u32[]{:S(2)}, u32[]{:S(2)}) async-start(f32[4,1,16384]{2,1,0:T(1,128)} %reshape.6), calls=%async_computation.1 | async-start | bytes 524288 | tf_op jit(solution)/shard_map/all_to_all | solution.py:104
  319.6 4.3 %all-to-all-done.1 = f32[4,1,16384]{2,1,0:T(1,128)S(1)} async-done(((f32[4,1,16384]{2,1,0:T(1,128)}), f32[4,1,16384]{2,1,0:T(1,128)S(1)}, u32[]{:S(2)}, u32[]{:S(2)}) %all-to-all-start.1) | async-done | bytes 262176 | tf_op jit(solution)/shard_map/all_to_all | solution.py:104
  326.8 12.7 %collective-permute-start.2 = (f32[1,128,128]{1,2,0:T(8,128)S(1)}, f32[1,128,128]{1,2,0:T(8,128)S(1)}, u32[]{:S(2)}, u32[]{:S(2)}) collective-permute-start(f32[1,128,128]{1,2,0:T(8,128)S(1)} %bitcast.60), channel_id=1, source_target_pairs={{4,0},{8,4},{12,8},{16,12},{20,16},{24,20},{28,24},{5,1},{9,5},{13... | collective-permute-start | bytes 196616 | tf_op jit(solution)/shard_map/ppermute | solution.py:16
  339.5 1.9 collective-permute-start.3
  341.8 4.7 %collective-permute-done.3 = f32[1,128,128]{1,2,0:T(8,128)S(1)} collective-permute-done((f32[1,128,128]{1,2,0:T(8,128)S(1)}, f32[1,128,128]{1,2,0:T(8,128)S(1)}, u32[]{:S(2)}, u32[]{:S(2)}) %collective-permute-start.3) | collective-permute-done | bytes 65568 | tf_op jit(solution)/shard_map/ppermute | solution.py:15
  346.8 1.9 collective-permute-start.4
  348.7 2.4 collective-permute-start.5
  351.2 2.8 collective-permute-done.4
  354.0 3.8 collective-permute-done.5
  358.1 3.4 collective-permute-start.10
  361.5 2.5 collective-permute-start.11
  364.1 1.9 collective-permute-start.8
  366.1 2.4 collective-permute-start.9
  368.8 3.1 collective-permute-start.12
  371.9 1.9 collective-permute-start.13
  375.2 2.0 collective-permute-done.12
  377.2 3.8 collective-permute-done.13
  383.5 6.5 %all-reduce.7 = (f32[]{:T(128)}, f32[]{:T(128)}, f32[]{:T(128)}, f32[]{:T(128)}, f32[]{:T(128)}, /*index=5*/f32[]{:T(128)}, f32[]{:T(128)}, f32[]{:T(128)}) all-reduce(f32[]{:T(128)} %get-tuple-element.434, f32[]{:T(128)} %multiply_reduce_fusion.8, f32[]{:T(128)} %get-tuple-element.433, ...), channel_id=1, replica_groups=mesh['layer'=8,'split'=4] {'split'}, use_global_device_ids=true, to_apply=%region_19.20 | all-reduce | flops 8 | bytes 64 | tf_op jit(solution)/shard_map/psum | solution.py:119
  390.0 17.5 %all-reduce.6 = (f32[]{:T(128)}, f32[]{:T(128)}, f32[]{:T(128)}, f32[]{:T(128)}, f32[]{:T(128)}, /*index=5*/f32[]{:T(128)}, f32[]{:T(128)}, f32[]{:T(128)}) all-reduce(f32[]{:T(128)} %get-tuple-element.488, f32[]{:T(128)} %get-tuple-element.489, f32[]{:T(128)} %get-tuple-element.490, ...), channel_id=1, replica_groups=mesh['layer'=8,'split'=4] {'layer'}, use_global_device_ids=true, to_apply=%region_20.21 | all-reduce | flops 8 | bytes 64 | tf_op jit(solution)/shard_map/psum | solution.py:119
  (121 shorter events, 50.3 us)
Async XLA Ops:
  7.2 37.6 %all-gather.2.cloned.1.call-start = ((), (), s32[]{:S(2)}) async-start(), calls=%async_computation.2 | async-start | bytes 5242880 | tf_op jit(solution)/shard_map/all_gather | solution.py:87
  9.7 13.6 %all-to-all-start = ((f32[4,128,128]{1,0,2:T(4,128)}), f32[4,128,128]{1,0,2:T(4,128)S(1)}, u32[]{:S(2)}, u32[]{:S(2)}) async-start(f32[4,128,128]{1,0,2:T(4,128)} %copy.44), calls=%async_computation | async-start | bytes 524288 | tf_op jit(solution)/shard_map/all_to_all | solution.py:88
  14.7 326.8 %collective-permute-start.6 = (f32[1,128,128]{1,2,0:T(8,128)S(1)}, f32[1,128,128]{1,2,0:T(8,128)S(1)}, u32[]{:S(2)}, u32[]{:S(2)}) collective-permute-start(f32[1,128,128]{1,2,0:T(8,128)S(1)} %get-tuple-element.515), channel_id=1, source_target_pairs={{4,0},{8,4},{12,8},{16,12},{20,16},{24,20},{28,24},{5,1},{9,5},{13... | collective-permute-start | bytes 196616 | tf_op jit(solution)/shard_map/ppermute | solution.py:16
  18.0 323.5 %collective-permute-start.7 = (f32[1,128,128]{1,2,0:T(8,128)S(1)}, f32[1,128,128]{1,2,0:T(8,128)S(1)}, u32[]{:S(2)}, u32[]{:S(2)}) collective-permute-start(f32[1,128,128]{1,2,0:T(8,128)S(1)} %get-tuple-element.514), channel_id=1, source_target_pairs={{0,4},{4,8},{8,12},{12,16},{16,20},{20,24},{24,28},{1,5},{5,9},{9,... | collective-permute-start | bytes 196616 | tf_op jit(solution)/shard_map/ppermute | solution.py:15
  45.5 7.0 %collective-permute-start.1 = (f32[512,32]{0,1:T(8,128)S(1)}, f32[512,32]{0,1:T(8,128)S(1)}, u32[]{:S(2)}, u32[]{:S(2)}) collective-permute-start(f32[512,32]{0,1:T(8,128)S(1)} %get-tuple-element.651), channel_id=1, source_target_pairs={{0,4},{4,8},{8,12},{12,16},{16,20},{20,24},{24,28},{1,5},{5,9},{9,... | collective-permute-start | bytes 196616 | tf_op jit(solution)/shard_map/while/body/eval_jaxpr/ppermute | solution.py:24
  53.3 24.6 %collective-permute-start.1 = (f32[512,32]{0,1:T(8,128)S(1)}, f32[512,32]{0,1:T(8,128)S(1)}, u32[]{:S(2)}, u32[]{:S(2)}) collective-permute-start(f32[512,32]{0,1:T(8,128)S(1)} %get-tuple-element.651), channel_id=1, source_target_pairs={{0,4},{4,8},{8,12},{12,16},{16,20},{20,24},{24,28},{1,5},{5,9},{9,... | collective-permute-start | bytes 196616 | tf_op jit(solution)/shard_map/while/body/eval_jaxpr/ppermute | solution.py:24
  89.6 7.1 %collective-permute-start.1 = (f32[512,32]{0,1:T(8,128)S(1)}, f32[512,32]{0,1:T(8,128)S(1)}, u32[]{:S(2)}, u32[]{:S(2)}) collective-permute-start(f32[512,32]{0,1:T(8,128)S(1)} %get-tuple-element.651), channel_id=1, source_target_pairs={{0,4},{4,8},{8,12},{12,16},{16,20},{20,24},{24,28},{1,5},{5,9},{9,... | collective-permute-start | bytes 196616 | tf_op jit(solution)/shard_map/while/body/eval_jaxpr/ppermute | solution.py:24
  97.4 13.9 %collective-permute-start.1 = (f32[512,32]{0,1:T(8,128)S(1)}, f32[512,32]{0,1:T(8,128)S(1)}, u32[]{:S(2)}, u32[]{:S(2)}) collective-permute-start(f32[512,32]{0,1:T(8,128)S(1)} %get-tuple-element.651), channel_id=1, source_target_pairs={{0,4},{4,8},{8,12},{12,16},{16,20},{20,24},{24,28},{1,5},{5,9},{9,... | collective-permute-start | bytes 196616 | tf_op jit(solution)/shard_map/while/body/eval_jaxpr/ppermute | solution.py:24
  112.0 7.0 %collective-permute-start.1 = (f32[512,32]{0,1:T(8,128)S(1)}, f32[512,32]{0,1:T(8,128)S(1)}, u32[]{:S(2)}, u32[]{:S(2)}) collective-permute-start(f32[512,32]{0,1:T(8,128)S(1)} %get-tuple-element.651), channel_id=1, source_target_pairs={{0,4},{4,8},{8,12},{12,16},{16,20},{20,24},{24,28},{1,5},{5,9},{9,... | collective-permute-start | bytes 196616 | tf_op jit(solution)/shard_map/while/body/eval_jaxpr/ppermute | solution.py:24
  119.8 14.8 %collective-permute-start.1 = (f32[512,32]{0,1:T(8,128)S(1)}, f32[512,32]{0,1:T(8,128)S(1)}, u32[]{:S(2)}, u32[]{:S(2)}) collective-permute-start(f32[512,32]{0,1:T(8,128)S(1)} %get-tuple-element.651), channel_id=1, source_target_pairs={{0,4},{4,8},{8,12},{12,16},{16,20},{20,24},{24,28},{1,5},{5,9},{9,... | collective-permute-start | bytes 196616 | tf_op jit(solution)/shard_map/while/body/eval_jaxpr/ppermute | solution.py:24
  135.3 7.0 %collective-permute-start.1 = (f32[512,32]{0,1:T(8,128)S(1)}, f32[512,32]{0,1:T(8,128)S(1)}, u32[]{:S(2)}, u32[]{:S(2)}) collective-permute-start(f32[512,32]{0,1:T(8,128)S(1)} %get-tuple-element.651), channel_id=1, source_target_pairs={{0,4},{4,8},{8,12},{12,16},{16,20},{20,24},{24,28},{1,5},{5,9},{9,... | collective-permute-start | bytes 196616 | tf_op jit(solution)/shard_map/while/body/eval_jaxpr/ppermute | solution.py:24
  143.1 13.9 %collective-permute-start.1 = (f32[512,32]{0,1:T(8,128)S(1)}, f32[512,32]{0,1:T(8,128)S(1)}, u32[]{:S(2)}, u32[]{:S(2)}) collective-permute-start(f32[512,32]{0,1:T(8,128)S(1)} %get-tuple-element.651), channel_id=1, source_target_pairs={{0,4},{4,8},{8,12},{12,16},{16,20},{20,24},{24,28},{1,5},{5,9},{9,... | collective-permute-start | bytes 196616 | tf_op jit(solution)/shard_map/while/body/eval_jaxpr/ppermute | solution.py:24
  157.7 7.4 %collective-permute-start = (f32[512,32]{0,1:T(8,128)S(1)}, f32[512,32]{0,1:T(8,128)S(1)}, u32[]{:S(2)}, u32[]{:S(2)}) collective-permute-start(f32[512,32]{0,1:T(8,128)S(1)} %get-tuple-element.659), channel_id=1, source_target_pairs={{4,0},{8,4},{12,8},{16,12},{20,16},{24,20},{28,24},{5,1},{9,5},{13... | collective-permute-start | bytes 196616 | tf_op jit(solution)/shard_map/while/body/eval_jaxpr/ppermute | solution.py:24
  165.9 15.7 %collective-permute-start = (f32[512,32]{0,1:T(8,128)S(1)}, f32[512,32]{0,1:T(8,128)S(1)}, u32[]{:S(2)}, u32[]{:S(2)}) collective-permute-start(f32[512,32]{0,1:T(8,128)S(1)} %get-tuple-element.659), channel_id=1, source_target_pairs={{4,0},{8,4},{12,8},{16,12},{20,16},{24,20},{28,24},{5,1},{9,5},{13... | collective-permute-start | bytes 196616 | tf_op jit(solution)/shard_map/while/body/eval_jaxpr/ppermute | solution.py:24
  182.4 7.0 %collective-permute-start = (f32[512,32]{0,1:T(8,128)S(1)}, f32[512,32]{0,1:T(8,128)S(1)}, u32[]{:S(2)}, u32[]{:S(2)}) collective-permute-start(f32[512,32]{0,1:T(8,128)S(1)} %get-tuple-element.659), channel_id=1, source_target_pairs={{4,0},{8,4},{12,8},{16,12},{20,16},{24,20},{28,24},{5,1},{9,5},{13... | collective-permute-start | bytes 196616 | tf_op jit(solution)/shard_map/while/body/eval_jaxpr/ppermute | solution.py:24
  190.1 14.0 %collective-permute-start = (f32[512,32]{0,1:T(8,128)S(1)}, f32[512,32]{0,1:T(8,128)S(1)}, u32[]{:S(2)}, u32[]{:S(2)}) collective-permute-start(f32[512,32]{0,1:T(8,128)S(1)} %get-tuple-element.659), channel_id=1, source_target_pairs={{4,0},{8,4},{12,8},{16,12},{20,16},{24,20},{28,24},{5,1},{9,5},{13... | collective-permute-start | bytes 196616 | tf_op jit(solution)/shard_map/while/body/eval_jaxpr/ppermute | solution.py:24
  204.8 64.4 %collective-permute-start = (f32[512,32]{0,1:T(8,128)S(1)}, f32[512,32]{0,1:T(8,128)S(1)}, u32[]{:S(2)}, u32[]{:S(2)}) collective-permute-start(f32[512,32]{0,1:T(8,128)S(1)} %get-tuple-element.659), channel_id=1, source_target_pairs={{4,0},{8,4},{12,8},{16,12},{20,16},{24,20},{28,24},{5,1},{9,5},{13... | collective-permute-start | bytes 196616 | tf_op jit(solution)/shard_map/while/body/eval_jaxpr/ppermute | solution.py:24
  281.7 6.2 %collective-permute-start = (f32[512,32]{0,1:T(8,128)S(1)}, f32[512,32]{0,1:T(8,128)S(1)}, u32[]{:S(2)}, u32[]{:S(2)}) collective-permute-start(f32[512,32]{0,1:T(8,128)S(1)} %get-tuple-element.659), channel_id=1, source_target_pairs={{4,0},{8,4},{12,8},{16,12},{20,16},{24,20},{28,24},{5,1},{9,5},{13... | collective-permute-start | bytes 196616 | tf_op jit(solution)/shard_map/while/body/eval_jaxpr/ppermute | solution.py:24
  288.5 16.4 %collective-permute-start = (f32[512,32]{0,1:T(8,128)S(1)}, f32[512,32]{0,1:T(8,128)S(1)}, u32[]{:S(2)}, u32[]{:S(2)}) collective-permute-start(f32[512,32]{0,1:T(8,128)S(1)} %get-tuple-element.659), channel_id=1, source_target_pairs={{4,0},{8,4},{12,8},{16,12},{20,16},{24,20},{28,24},{5,1},{9,5},{13... | collective-permute-start | bytes 196616 | tf_op jit(solution)/shard_map/while/body/eval_jaxpr/ppermute | solution.py:24
  305.7 7.0 %collective-permute-start = (f32[512,32]{0,1:T(8,128)S(1)}, f32[512,32]{0,1:T(8,128)S(1)}, u32[]{:S(2)}, u32[]{:S(2)}) collective-permute-start(f32[512,32]{0,1:T(8,128)S(1)} %get-tuple-element.659), channel_id=1, source_target_pairs={{4,0},{8,4},{12,8},{16,12},{20,16},{24,20},{28,24},{5,1},{9,5},{13... | collective-permute-start | bytes 196616 | tf_op jit(solution)/shard_map/while/body/eval_jaxpr/ppermute | solution.py:24
  314.5 9.4 %all-to-all-start.1 = ((f32[4,1,16384]{2,1,0:T(1,128)}), f32[4,1,16384]{2,1,0:T(1,128)S(1)}, u32[]{:S(2)}, u32[]{:S(2)}) async-start(f32[4,1,16384]{2,1,0:T(1,128)} %reshape.6), calls=%async_computation.1 | async-start | bytes 524288 | tf_op jit(solution)/shard_map/all_to_all | solution.py:104
  326.8 15.1 %collective-permute-start.2 = (f32[1,128,128]{1,2,0:T(8,128)S(1)}, f32[1,128,128]{1,2,0:T(8,128)S(1)}, u32[]{:S(2)}, u32[]{:S(2)}) collective-permute-start(f32[1,128,128]{1,2,0:T(8,128)S(1)} %bitcast.60), channel_id=1, source_target_pairs={{4,0},{8,4},{12,8},{16,12},{20,16},{24,20},{28,24},{5,1},{9,5},{13... | collective-permute-start | bytes 196616 | tf_op jit(solution)/shard_map/ppermute | solution.py:16
  339.5 7.1 %collective-permute-start.3 = (f32[1,128,128]{1,2,0:T(8,128)S(1)}, f32[1,128,128]{1,2,0:T(8,128)S(1)}, u32[]{:S(2)}, u32[]{:S(2)}) collective-permute-start(f32[1,128,128]{1,2,0:T(8,128)S(1)} %bitcast.61), channel_id=1, source_target_pairs={{0,4},{4,8},{8,12},{12,16},{16,20},{20,24},{24,28},{1,5},{5,9},{9,... | collective-permute-start | bytes 196616 | tf_op jit(solution)/shard_map/ppermute | solution.py:15
  346.8 7.2 %collective-permute-start.4 = (f32[6,1,128]{1,2,0:T(8,128)S(1)}, f32[6,1,128]{1,2,0:T(8,128)S(1)}, u32[]{:S(2)}, u32[]{:S(2)}) collective-permute-start(f32[6,1,128]{1,2,0:T(8,128)S(1)} %get-tuple-element.508), channel_id=1, source_target_pairs={{1,0},{2,1},{3,2},{5,4},{6,5},{7,6},{9,8},{10,9},{11,10},{13,12},{... | collective-permute-start | bytes 9224 | tf_op jit(solution)/shard_map/ppermute | solution.py:16
  348.7 9.1 %collective-permute-start.5 = (f32[6,1,128]{1,2,0:T(8,128)S(1)}, f32[6,1,128]{1,2,0:T(8,128)S(1)}, u32[]{:S(2)}, u32[]{:S(2)}) collective-permute-start(f32[6,1,128]{1,2,0:T(8,128)S(1)} %get-tuple-element.509), channel_id=1, source_target_pairs={{0,1},{1,2},{2,3},{4,5},{5,6},{6,7},{8,9},{9,10},{10,11},{12,13},{... | collective-permute-start | bytes 9224 | tf_op jit(solution)/shard_map/ppermute | solution.py:15
  358.1 10.4 %collective-permute-start.10 = (f32[1,128,128]{1,2,0:T(8,128)S(1)}, f32[1,128,128]{1,2,0:T(8,128)S(1)}, u32[]{:S(2)}, u32[]{:S(2)}) collective-permute-start(f32[1,128,128]{1,2,0:T(8,128)S(1)} %get-tuple-element.511), channel_id=1, source_target_pairs={{4,0},{8,4},{12,8},{16,12},{20,16},{24,20},{28,24},{5,1},{9,5},{13... | collective-permute-start | bytes 196616 | tf_op jit(solution)/shard_map/ppermute | solution.py:16
  361.5 7.1 %collective-permute-start.11 = (f32[1,128,128]{1,2,0:T(8,128)S(1)}, f32[1,128,128]{1,2,0:T(8,128)S(1)}, u32[]{:S(2)}, u32[]{:S(2)}) collective-permute-start(f32[1,128,128]{1,2,0:T(8,128)S(1)} %get-tuple-element.510), channel_id=1, source_target_pairs={{0,4},{4,8},{8,12},{12,16},{16,20},{20,24},{24,28},{1,5},{5,9},{9,... | collective-permute-start | bytes 196616 | tf_op jit(solution)/shard_map/ppermute | solution.py:15
  364.1 9.7 %collective-permute-start.8 = (f32[6,1,128]{1,2,0:T(8,128)S(1)}, f32[6,1,128]{1,2,0:T(8,128)S(1)}, u32[]{:S(2)}, u32[]{:S(2)}) collective-permute-start(f32[6,1,128]{1,2,0:T(8,128)S(1)} %get-tuple-element.506), channel_id=1, source_target_pairs={{1,0},{2,1},{3,2},{5,4},{6,5},{7,6},{9,8},{10,9},{11,10},{13,12},{... | collective-permute-start | bytes 9224 | tf_op jit(solution)/shard_map/ppermute | solution.py:16
  366.1 9.1 %collective-permute-start.9 = (f32[6,1,128]{1,2,0:T(8,128)S(1)}, f32[6,1,128]{1,2,0:T(8,128)S(1)}, u32[]{:S(2)}, u32[]{:S(2)}) collective-permute-start(f32[6,1,128]{1,2,0:T(8,128)S(1)} %get-tuple-element.507), channel_id=1, source_target_pairs={{0,1},{1,2},{2,3},{4,5},{5,6},{6,7},{8,9},{9,10},{10,11},{12,13},{... | collective-permute-start | bytes 9224 | tf_op jit(solution)/shard_map/ppermute | solution.py:15
  368.8 8.4 %collective-permute-start.12 = (f32[6,1,128]{1,2,0:T(8,128)S(1)}, f32[6,1,128]{1,2,0:T(8,128)S(1)}, u32[]{:S(2)}, u32[]{:S(2)}) collective-permute-start(f32[6,1,128]{1,2,0:T(8,128)S(1)} %get-tuple-element.504), channel_id=1, source_target_pairs={{1,0},{2,1},{3,2},{5,4},{6,5},{7,6},{9,8},{10,9},{11,10},{13,12},{... | collective-permute-start | bytes 9224 | tf_op jit(solution)/shard_map/ppermute | solution.py:16
  371.9 9.1 %collective-permute-start.13 = (f32[6,1,128]{1,2,0:T(8,128)S(1)}, f32[6,1,128]{1,2,0:T(8,128)S(1)}, u32[]{:S(2)}, u32[]{:S(2)}) collective-permute-start(f32[6,1,128]{1,2,0:T(8,128)S(1)} %get-tuple-element.505), channel_id=1, source_target_pairs={{0,1},{1,2},{2,3},{4,5},{5,6},{6,7},{8,9},{9,10},{10,11},{12,13},{... | collective-permute-start | bytes 9224 | tf_op jit(solution)/shard_map/ppermute | solution.py:15
Sparse Core Ops, SparseCore 0:
  9.5 35.1 all-gather.1
